TPU v7x, 8 devices: a whole 2x2x1 slice. The times are simulated.
8 devices in a mesh: rep: 2 (over z, y), dp: 4 (over x, core).
Axes of the slice: x: 2, y: 2, z: 1, core: 2. Of those that a mesh axis runs over, the one named last changes fastest.
Arguments:
- hidden: bfloat16 [256, 2048], P(('rep', 'dp')), parts along dimension 0
- lengths: int32 [256], P(('rep', 'dp')), parts along dimension 0
- kv_cache: bfloat16 [2, 256, 128, 576], P(None, ('rep', 'dp')), parts along dimension 1
- norm_attn: float32 [2, 2048], replicated
- w_q: bfloat16 [2, 2048, 9216], replicated
- w_o: bfloat16 [2, 8192, 2048], replicated
- norm_ffn: float32 [2, 2048], replicated
- w_gate: bfloat16 [2, 2048, 10944], P(None, None, 'dp')
- w_up: bfloat16 [2, 2048, 10944], P(None, None, 'dp')
- w_down: bfloat16 [2, 10944, 2048], P(None, 'dp')
- norm_final: float32 [2048], replicated
- w_head: bfloat16 [2048, 102400], P(None, 'dp')
Outputs:
- output: float32 [256, 102400], P('rep', 'dp'), parts along dimension 0
There are 2 independent parts. A program takes and returns all parts, laid end to end along the dimension named above; an argument that names none is the same for every part.
All inputs are finite; a program needn't handle non-finite values.
Results may differ from a plain program's by a relative error of at most 0.02.
Values are sent between devices in bfloat16 or wider.
A program may use at most 1.5 GiB of HBM per device.

v0:
```python
import functools

import jax
import jax.numpy as jnp
from jax import lax
from jax.experimental import pallas as pl
from jax.experimental.pallas import tpu as pltpu
from jax.sharding import PartitionSpec as P

F32 = jnp.float32
BF16 = jnp.bfloat16
MESH = pl.DeviceIdType.MESH

D = 2048
HEADS = 16
LATENT = 512
KV_W = 576
SEQ = 128
ROWS = 32
CHIP = 64
ALL = 128
FFN = 2736
FFN_PAD = 2816
NC = 512
QH = HEADS * KV_W // 2
PAIR = 2 * KV_W
VOCAB = 25600
QK_SCALE = 192 ** -0.5
NORM_EPS = 1e-6
LAYERS = 2


def _rows_norm(chunks, gain, dtype=BF16):
    ss = sum(jnp.sum(v * v, axis=-1, keepdims=True) for v in chunks)
    inv = lax.rsqrt(ss * (1.0 / D) + NORM_EPS)
    return [(v * inv * gain[:, i * NC:(i + 1) * NC]).astype(dtype) for i, v in enumerate(chunks)]


def body(hid_h, lens_h, ga_h, gf_h, gl_h, kv, wq, wo, wg, wu, wd, wh, H, S, G, DN,
         hid, lens, ga, gf, gl, in_sem, KV, X, Qf, Qs, O16, A, PS, CS, R1, R2,
         s_sem, g_sem, d_sem, kv_sem, q_ss, q_rs, o_ss, o_rs, ad_ss, ad_rs, al_ss, al_rs, af_ss, af_rs,
         p_ss, p_rs, c_ss, c_rs, h_ss, h_rs):
    me = lax.axis_index('dp')
    c = lax.rem(me, 2)
    chip = me // 2
    partner = me + 1 - 2 * c
    other = lax.rem(me + 2, 4)
    my_row = pl.multiple_of(me * ROWS, ROWS)
    pa_row = pl.multiple_of(partner * ROWS, ROWS)
    chip_row = pl.multiple_of(chip * CHIP, CHIP)
    oth_row = pl.multiple_of((1 - chip) * CHIP, CHIP)

    def rdma(src, dst, ss, rs, dev):
        return pltpu.make_async_remote_copy(src_ref=src, dst_ref=dst, send_sem=ss, recv_sem=rs,
                                            device_id={'dp': dev}, device_id_type=MESH)

    def cp_wq(l, i):
        p, kk = i // 2, i % 2
        col = pl.multiple_of(c * QH + p * PAIR, 128)
        return pltpu.make_async_copy(wq.at[l, pl.ds(kk * 1024, 1024), pl.ds(col, PAIR)], S.at[i], s_sem.at[i])

    def cp_wo(l, i):
        col = pl.multiple_of(c * 1024, 128)
        return pltpu.make_async_copy(wo.at[l, pl.ds(i * 1024, 1024), pl.ds(col, 1024)],
                                     S.at[i, :, pl.ds(0, 1024)], s_sem.at[i])

    def cp_g(l, i):
        w, j = i // 6, i % 6
        src = wg if w == 0 else wu
        return pltpu.make_async_copy(src.at[l, pl.ds(j * 456, 456), :], G.at[w, pl.ds(j * 456, 456), :], g_sem.at[i])

    def dn_col(i):
        owner = 1 - c if i % 2 == 0 else c
        return 2 * owner + i // 2

    def cp_d(l, i):
        col = pl.multiple_of(dn_col(i) * NC, NC)
        return pltpu.make_async_copy(wd.at[l, :, pl.ds(col, NC)], DN.at[i, pl.ds(0, FFN), :], d_sem.at[i])

    def cp_kv(l, i):
        return pltpu.make_async_copy(kv.at[l, pl.ds(i * 8, 8)], KV.at[pl.ds(i * 8, 8)], kv_sem.at[i])

    def cp_hs(i):
        return pltpu.make_async_copy(wh.at[pl.ds((i % 2) * 1024, 1024), pl.ds((i // 2) * 1024, 1024)],
                                     S.at[i, :, pl.ds(0, 1024)], s_sem.at[i])

    def cp_hg(i):
        g, j = i // 4, i % 4
        return pltpu.make_async_copy(wh.at[pl.ds(j * 512, 512), pl.ds(4096 + g * D, D)],
                                     G.at[g, pl.ds(j * 512, 512), :], g_sem.at[i])

    def cp_hd(i):
        return pltpu.make_async_copy(wh.at[:, pl.ds(8192 + i * NC, NC)], DN.at[i, pl.ds(0, D), :], d_sem.at[i])

    ins = [pltpu.make_async_copy(a, b, in_sem.at[i]) for i, (a, b) in enumerate(
        ((hid_h, hid), (lens_h, lens), (ga_h, ga), (gf_h, gf), (gl_h, gl)))]
    for cp in ins:
        cp.start()
    for i in range(4):
        cp_wq(0, i).start()

    bar = pltpu.get_barrier_semaphore()
    for dev in (partner, other):
        pl.semaphore_signal(bar, inc=1, device_id={'dp': dev}, device_id_type=MESH)
    pl.semaphore_wait(bar, 2)

    ins[0].wait()
    for n in range(4):
        X[n, pl.ds(my_row, ROWS), :] = hid[:, n * NC:(n + 1) * NC]
    hx = rdma(X.at[:, pl.ds(my_row, ROWS), :], X.at[:, pl.ds(my_row, ROWS), :], h_ss.at[0], h_rs.at[0], partner)
    hx.start()
    for i in range(4):
        DN[i, FFN:FFN_PAD, :] = jnp.zeros((FFN_PAD - FFN, NC), BF16)
    A[:, FFN_PAD - 128:FFN_PAD] = jnp.zeros((ALL, 128), BF16)
    for cp in ins[1:]:
        cp.wait()
    hx.wait_send()
    rdma(X.at[:, pl.ds(pa_row, ROWS), :], X.at[:, pl.ds(pa_row, ROWS), :], h_ss.at[0], h_rs.at[0], partner).wait_recv()

    def x_chunks(row, rows):
        return [X[n, pl.ds(row, rows), :].astype(F32) for n in range(4)]

    def norm_to_h(row, rows, h_row, gain):
        for n, v in enumerate(_rows_norm(x_chunks(row, rows), gain)):
            H[pl.ds(h_row, rows), n * NC:(n + 1) * NC] = v

    def own_n(j):
        return 2 * c + j

    def par_n(j):
        return 2 * (1 - c) + j

    def ad(j, n):
        r = X.at[n, pl.ds(chip_row, CHIP), :]
        return rdma(r, r, ad_ss.at[j], ad_rs.at[j], partner)

    def al(j, row):
        r = X.at[own_n(j), pl.ds(row, CHIP), :]
        return rdma(r, r, al_ss.at[j], al_rs.at[j], other)

    def af(j, n):
        r = X.at[n, pl.ds(oth_row, CHIP), :]
        return rdma(r, r, af_ss.at[j], af_rs.at[j], partner)

    def gather_start(j):
        al(j, chip_row).start()
        ad(j, own_n(j)).start()

    def gather_finish():
        for j in range(2):
            al(j, oth_row).wait_recv()
            af(j, own_n(j)).start()
        for j in range(2):
            ad(j, par_n(j)).wait_recv()
        for j in range(2):
            af(j, par_n(j)).wait_recv()
        for j in range(2):
            al(j, chip_row).wait_send()
            ad(j, own_n(j)).wait_send()
            af(j, own_n(j)).wait_send()

    for l in range(LAYERS):
        norm_to_h(my_row, ROWS, 0, ga[l:l + 1, :])
        norm_to_h(pa_row, ROWS, ROWS, ga[l:l + 1, :])

        def q_send(p):
            dst = Qf.at[:, pl.ds(pl.multiple_of((c * 8 + 2 * p) * ROWS, ROWS), 2 * ROWS), :]
            return rdma(Qs.at[:, pl.ds(2 * p * ROWS, 2 * ROWS), :], dst, q_ss.at[p], q_rs.at[p], partner)

        def q_recv(p):
            dst = Qf.at[:, pl.ds(pl.multiple_of(((1 - c) * 8 + 2 * p) * ROWS, ROWS), 2 * ROWS), :]
            return rdma(dst, dst, q_ss.at[p], q_rs.at[p], partner)

        for p in range(4):
            cp_wq(l, 2 * p).wait()
            cp_wq(l, 2 * p + 1).wait()
            if l == 0:
                if p < 2:
                    cp_wq(0, 2 * p + 4).start()
                    cp_wq(0, 2 * p + 5).start()
                if p == 1:
                    for i in range(4):
                        cp_kv(0, i).start()
                if p == 2:
                    for i in range(4):
                        cp_wo(0, i).start()
            r = jnp.dot(H[0:CHIP, 0:1024], S[2 * p], preferred_element_type=F32)
            r = r + jnp.dot(H[0:CHIP, 1024:2048], S[2 * p + 1], preferred_element_type=F32)
            if l > 0 or p > 1:
                cp_wo(l, 2 * p).start()
                cp_wo(l, 2 * p + 1).start()
            r = r.astype(BF16).astype(F32)
            for j in range(2):
                rj = r[:, j * KV_W:(j + 1) * KV_W]
                row = pl.multiple_of((c * 8 + 2 * p + j) * ROWS, ROWS)
                rj = jnp.concatenate([rj, jnp.zeros((CHIP, 64), F32)], axis=1)
                for t in range(5):
                    v = rj[:, t * 128:(t + 1) * 128]
                    Qf[t, pl.ds(row, ROWS), :] = v[0:ROWS]
                    Qs[t, (2 * p + j) * ROWS:(2 * p + j + 1) * ROWS, :] = v[ROWS:CHIP]
            q_send(p).start()
        for p in range(4):
            q_recv(p).wait_recv()
        for p in range(4):
            q_send(p).wait_send()

        def o_send(g2):
            r0 = g2 * 16
            return rdma(O16.at[:, pl.ds(r0, 16), :], O16.at[:, pl.ds(ROWS + r0, 16), :],
                        o_ss.at[g2], o_rs.at[g2], partner)

        for g in range(4):
            cp_kv(l, g).wait()
            if l == 0 and g > 0:
                for i in range(4):
                    cp_g(0, 4 * (g - 1) + i).start()
            sc = []
            for i in range(8):
                b = g * 8 + i
                qb = jnp.concatenate([Qf[t, pl.ds(b, HEADS, stride=ROWS), :] for t in range(5)], axis=1)
                s = jnp.dot(qb[:, 0:KV_W].astype(BF16), KV[b], preferred_element_type=F32) * QK_SCALE
                pos = lax.broadcasted_iota(jnp.int32, (HEADS, SEQ), 1)
                sc.append(jnp.where(pos < lens[b], s, -1e30))
            s = jnp.concatenate(sc, axis=0)
            e = jnp.exp(s - jnp.max(s, axis=-1, keepdims=True))
            pr = (e / jnp.sum(e, axis=-1, keepdims=True)).astype(BF16)
            for i in range(8):
                b = g * 8 + i
                o = lax.dot_general(pr[i * HEADS:(i + 1) * HEADS], KV[b, 0:LATENT, :], (((1,), (1,)), ((), ())),
                                    preferred_element_type=F32)
                for t in range(4):
                    Qf[t, pl.ds(b, HEADS, stride=ROWS), :] = o[:, t * 128:(t + 1) * 128]
            if g % 2 == 1:
                r0 = (g // 2) * 16
                for h in range(HEADS):
                    for t in range(4):
                        O16[h, r0:r0 + 16, t * 128:(t + 1) * 128] = (
                            Qf[t, h * ROWS + r0:h * ROWS + r0 + 16, :].astype(BF16))
                o_send(g // 2).start()
        for g2 in range(2):
            r0 = g2 * 16
            ref = O16.at[:, pl.ds(ROWS + r0, 16), :]
            rdma(ref, ref, o_ss.at[g2], o_rs.at[g2], partner).wait_recv()
        for g2 in range(2):
            o_send(g2).wait_send()

        for i in range(8):
            cp_wo(l, i).wait()
        if l == 0:
            for i in range(4):
                cp_d(0, i).start()
        for j in range(2):
            acc = None
            for k in range(8):
                for hh in range(2):
                    t = jnp.dot(O16[2 * k + hh], S[k, hh * LATENT:(hh + 1) * LATENT, j * NC:(j + 1) * NC],
                                preferred_element_type=F32)
                    acc = t if acc is None else acc + t
            n = own_n(j)
            X[n, pl.ds(my_row, ROWS), :] = (X[n, pl.ds(my_row, ROWS), :].astype(F32) + acc[0:ROWS]).astype(BF16)
            X[n, pl.ds(pa_row, ROWS), :] = (X[n, pl.ds(pa_row, ROWS), :].astype(F32) + acc[ROWS:CHIP]).astype(BF16)
            gather_start(j)
        if l + 1 == LAYERS:
            for i in range(8):
                cp_hs(i).start()
        gather_finish()

        for r in range(4):
            norm_to_h(r * ROWS, ROWS, r * ROWS, gf[l:l + 1, :])
        if l + 1 < LAYERS:
            for i in range(8):
                cp_wq(l + 1, i).start()
            for i in range(4):
                cp_kv(l + 1, i).start()
        for i in range(12):
            cp_g(l, i).wait()

        def ffn_cols(n0, size):
            g_ = lax.dot_general(H[...], G[0, pl.ds(n0, size), :], (((1,), (1,)), ((), ())),
                                 preferred_element_type=F32)
            u_ = lax.dot_general(H[...], G[1, pl.ds(n0, size), :], (((1,), (1,)), ((), ())),
                                 preferred_element_type=F32)
            A[:, pl.ds(n0, size)] = (jax.nn.silu(g_) * u_).astype(BF16)

        def ffn_step(n, carry):
            ffn_cols(pl.multiple_of(n * NC, NC), NC)
            return carry

        lax.fori_loop(0, 5, ffn_step, 0)
        ffn_cols(5 * NC, FFN - 5 * NC)
        if l + 1 < LAYERS:
            for i in range(12):
                cp_g(l + 1, i).start()
        else:
            for i in range(8):
                cp_hg(i).start()

        def ps(j):
            return rdma(PS.at[j], R1.at[j], p_ss.at[j], p_rs.at[j], partner)

        def cs(j):
            return rdma(CS.at[j, pl.ds(oth_row, CHIP), :], R2.at[j], c_ss.at[j], c_rs.at[j], other)

        def down(i):
            cp_d(l, i).wait()
            y = jnp.dot(A[...], DN[i], preferred_element_type=F32)
            if l + 1 < LAYERS:
                cp_d(l + 1, i).start()
            else:
                cp_hd(i).start()
            return y

        def chip_sum(j):
            ps(j).wait_recv()
            CS[j] = CS[j] + R1[j]
            cs(j).start()

        PS[0] = down(0)
        ps(0).start()
        CS[0] = down(1)
        PS[1] = down(2)
        ps(1).start()
        chip_sum(0)
        CS[1] = down(3)
        chip_sum(1)
        last = l + 1 == LAYERS
        for j in range(2):
            cs(j).wait_recv()
            n = own_n(j)
            xr = X[n, pl.ds(chip_row, CHIP), :].astype(F32)
            X[n, pl.ds(chip_row, CHIP), :] = (xr + (CS[j, pl.ds(chip_row, CHIP), :] + R2[j])).astype(BF16)
            if last:
                gather_start(j)
            else:
                ad(j, own_n(j)).start()
        for j in range(2):
            ps(j).wait_send()
            cs(j).wait_send()
        if last:
            gather_finish()
        else:
            for j in range(2):
                ad(j, par_n(j)).wait_recv()
            for j in range(2):
                ad(j, own_n(j)).wait_send()

    for r in range(4):
        norm_to_h(r * ROWS, ROWS, r * ROWS, gl[...])
    for i in range(8):
        cp_hs(i).wait()
        cp_hg(i).wait()
    for i in range(4):
        cp_hd(i).wait()


RING = 4
BLOCKS = VOCAB // NC
HELD = 20
STREAM = BLOCKS - HELD


def head_body(H, S, G, DN, wh, out, W, OH, OS, w_sem, oh_sem, os_sem):
    def cp_w(t, slot):
        col = pl.multiple_of((HELD + t) * NC, NC)
        return pltpu.make_async_copy(wh.at[:, pl.ds(col, NC)], W.at[slot], w_sem.at[slot])

    def cp_out(buf, sems, block, slot):
        col = pl.multiple_of(block * NC, NC)
        return pltpu.make_async_copy(buf.at[slot], out.at[:, pl.ds(col, NC)], sems.at[slot])

    for t in range(RING):
        cp_w(t, t).start()

    def stream(t):
        slot, o = lax.rem(t, RING), lax.rem(t, 2)
        cp_w(t, slot).wait()

        @pl.when(t >= 2)
        def _():
            cp_out(OS, os_sem, HELD + t, o).wait()

        OS[o] = jnp.dot(H[...], W[slot], preferred_element_type=F32)
        cp_out(OS, os_sem, HELD + t, o).start()

        @pl.when(t + RING < STREAM)
        def _():
            cp_w(t + RING, slot).start()

    def held(t, value):
        o = lax.rem(t, 2)

        @pl.when(t >= 2)
        def _():
            cp_out(OH, oh_sem, t, o).wait()

        OH[o] = value()
        cp_out(OH, oh_sem, t, o).start()

    def dot(a, b):
        return jnp.dot(a, b, preferred_element_type=F32)

    def seg_s(t, carry):
        p, col = t // 2, pl.multiple_of(lax.rem(t, 2) * NC, NC)
        held(t, lambda: dot(H[:, 0:1024], S[2 * p, :, pl.ds(col, NC)])
             + dot(H[:, 1024:2048], S[2 * p + 1, :, pl.ds(col, NC)]))
        stream(t)
        return carry

    def seg_g(t, carry):
        g, col = t // 4 - 2, pl.multiple_of(lax.rem(t, 4) * NC, NC)
        held(t, lambda: dot(H[...], G[g, 0:D, pl.ds(col, NC)]))
        stream(t)
        return carry

    def seg_d(t, carry):
        held(t, lambda: dot(H[...], DN[t - 16, 0:D, :]))
        stream(t)
        return carry

    def seg_w(t, carry):
        stream(t)
        return carry

    lax.fori_loop(0, 8, seg_s, 0)
    lax.fori_loop(8, 16, seg_g, 0)
    lax.fori_loop(16, 20, seg_d, 0)
    lax.fori_loop(20, STREAM, seg_w, 0)
    for o in range(2):
        cp_out(OH, oh_sem, HELD - 2 + o, o).wait()
        cp_out(OS, os_sem, BLOCKS - 2 + o, o).wait()


def head_kernel(normed, s_buf, g_buf, d_buf, w_head):
    vm = pl.BlockSpec(memory_space=pltpu.VMEM)
    hb = pl.BlockSpec(memory_space=pl.ANY)
    dma = pltpu.SemaphoreType.DMA
    held = [pltpu.with_memory_space_constraint(a, pltpu.VMEM) for a in (normed, s_buf, g_buf, d_buf)]
    return pl.pallas_call(
        head_body,
        out_shape=jax.ShapeDtypeStruct((ALL, VOCAB), F32),
        in_specs=[vm] * 4 + [hb],
        out_specs=hb,
        scratch_shapes=[pltpu.VMEM((RING, D, NC), BF16), pltpu.VMEM((2, ALL, NC), F32), pltpu.VMEM((2, ALL, NC), F32),
                        dma((RING,)), dma((2,)), dma((2,))],
        compiler_params=pltpu.CompilerParams(vmem_limit_bytes=13500000),
        name='head',
    )(*held, w_head)


def layers_kernel(hidden, lengths, kv_t, norm_attn, w_q, w_o, norm_ffn, wg_t, wu_t, w_down, norm_final, w_head):
    hb = pl.BlockSpec(memory_space=pl.ANY)
    dma = pltpu.SemaphoreType.DMA
    vm = pl.BlockSpec(memory_space=pltpu.VMEM)
    scratch = [
        pltpu.VMEM((ROWS, D), BF16), pltpu.SMEM((ROWS,), jnp.int32), pltpu.VMEM((2, D), F32), pltpu.VMEM((2, D), F32),
        pltpu.VMEM((1, D), F32), dma((5,)),
        pltpu.VMEM((ROWS, KV_W, SEQ), BF16),
        pltpu.VMEM((4, ALL, NC), BF16),
        pltpu.VMEM((5, HEADS * ROWS, 128), F32),
        pltpu.VMEM((5, 8 * ROWS, 128), F32),
        pltpu.VMEM((HEADS, CHIP, LATENT), BF16),
        pltpu.VMEM((ALL, FFN_PAD), BF16),
        pltpu.VMEM((2, ALL, NC), F32),
        pltpu.VMEM((2, ALL, NC), F32),
        pltpu.VMEM((2, ALL, NC), F32),
        pltpu.VMEM((2, CHIP, NC), F32),
        dma((8,)), dma((12,)), dma((4,)), dma((4,)),
        dma((4,)), dma((4,)), dma((2,)), dma((2,)),
        dma((2,)), dma((2,)), dma((2,)), dma((2,)), dma((2,)), dma((2,)),
        dma((2,)), dma((2,)), dma((2,)), dma((2,)), dma((1,)), dma((1,)),
    ]
    return pl.pallas_call(
        body,
        out_shape=[pltpu.VMEM((ALL, D), BF16), pltpu.VMEM((8, 1024, PAIR), BF16), pltpu.VMEM((2, FFN, D), BF16),
                   pltpu.VMEM((4, FFN_PAD, NC), BF16)],
        in_specs=[hb] * 12,
        out_specs=[vm] * 4,
        scratch_shapes=scratch,
        compiler_params=pltpu.CompilerParams(collective_id=0, has_side_effects=True, vmem_limit_bytes=13500000),
        name='layers',
    )(hidden, lengths, norm_attn, norm_ffn, norm_final.reshape(1, D), kv_t, w_q, w_o, wg_t, wu_t, w_down, w_head)


def solution(mesh):
    row_axes = ('rep', 'dp')
    specs_in = (P(row_axes, None), P(row_axes), P(None, row_axes, None, None), P(), P(), P(), P(),
                P(None, None, 'dp'), P(None, None, 'dp'), P(None, 'dp', None), P(), P(None, 'dp'))

    def device_step(hidden, lengths, kv_cache, norm_attn, w_q, w_o, norm_ffn, w_gate, w_up, w_down, norm_final, w_head):
        held = layers_kernel(hidden, lengths, jnp.swapaxes(kv_cache, 2, 3), norm_attn, w_q, w_o, norm_ffn,
                               jnp.swapaxes(w_gate, 1, 2), jnp.swapaxes(w_up, 1, 2), w_down, norm_final, w_head)
        return head_kernel(*held, w_head)

    return jax.shard_map(device_step, mesh=mesh, in_specs=specs_in, out_specs=P('rep', 'dp'), check_vma=False)
```

profile of v0, /device:TPU:0, one launch (start us, length us, event | category | flops | bytes accessed | tf_op | source)
XLA Modules:
  0.0 111.3 jit_solution(10910975712120776082)
XLA Ops:
  0.0 84.3 %layers.1 = (bf16[128,2048]{1,0:T(8,128)(2,1)S(1)}, bf16[8,1024,1152]{2,1,0:T(8,128)(2,1)S(1)}, bf16[2,2736,2048]{2,1,0:T(8,128)(2,1)S(1)}, bf16[4,2816,512]{2,1,0:T(8,128)(2,1)S(1)}) custom-call(bf16[32,2048]{1,0:T(8,128)(2,1)} %hid_h.1, s32[32]{0:T(128)} %lens_h.1, f32[2,2048]{1,0:T(2,128)} %ga_h.1, f32[2,2048]{1,0:T(2,128)} %gf_h.1, f32[1,2048]{1,0:T(1,128)} %bitcast.7, ...), custom_call_target="tpu_custom_call" | custom-call | tf_op jit(solution)/shard_map/layers/pallas_call | solution.py:472
  84.3 26.8 %head.1 = f32[128,25600]{1,0:T(8,128)} custom-call(bf16[128,2048]{1,0:T(8,128)(2,1)S(1)} %get-tuple-element.9.H, bf16[8,1024,1152]{2,1,0:T(8,128)(2,1)S(1)} %get-tuple-element.10.S, bf16[2,2736,2048]{2,1,0:T(8,128)(2,1)S(1)} %get-tuple-element.11.G, bf16[4,2816,512]{2,1,0:T(8,128)(2,1)S(1)} %get-tuple-element.12.DN, bf16[2048,25600]{1,0:T(8,128)(2,1)} %wh.3), custom_call_target="tpu_custom_call" | custom-call | tf_op jit(solution)/shard_map/head/pallas_call | solution.py:438
where the time goes:
time: 111 us
  Pallas kernels  111 us (100%)
    pallas_call x1, Pallas kernels, layers_kernel(): pl.pallas_call(body, out_shape=[pltpu.VMEM((ALL, D), BF16), pltpu.VMEM((8...  84.3 us
    pallas_call x1, Pallas kernels, head_kernel(): pl.pallas_call(head_body, out_shape=jax.ShapeDtypeStruct((ALL, VOCAB), F3...  26.8 us

commit v1 on v0

--- a/solution.py
+++ b/solution.py
@@ -39,7 +39,7 @@
 def body(hid_h, lens_h, ga_h, gf_h, gl_h, kv, wq, wo, wg, wu, wd, wh, H, S, G, DN,
          hid, lens, ga, gf, gl, in_sem, KV, X, Qf, Qs, O16, A, PS, CS, R1, R2,
          s_sem, g_sem, d_sem, kv_sem, q_ss, q_rs, o_ss, o_rs, ad_ss, ad_rs, al_ss, al_rs, af_ss, af_rs,
-         p_ss, p_rs, c_ss, c_rs, h_ss, h_rs):
+         p_ss, p_rs, c_ss, c_rs, h_ss, h_rs, x_sem):
     me = lax.axis_index('dp')
     c = lax.rem(me, 2)
     chip = me // 2
@@ -65,9 +65,10 @@
                                      S.at[i, :, pl.ds(0, 1024)], s_sem.at[i])
 
     def cp_g(l, i):
-        w, j = i // 6, i % 6
+        w, j = i % 2, i // 2
         src = wg if w == 0 else wu
-        return pltpu.make_async_copy(src.at[l, pl.ds(j * 456, 456), :], G.at[w, pl.ds(j * 456, 456), :], g_sem.at[i])
+        rows = NC if j < 5 else FFN - 5 * NC
+        return pltpu.make_async_copy(src.at[l, pl.ds(j * NC, rows), :], G.at[w, pl.ds(j * NC, rows), :], g_sem.at[i])
 
     def dn_col(i):
         owner = 1 - c if i % 2 == 0 else c
@@ -91,6 +92,14 @@
 
     def cp_hd(i):
         return pltpu.make_async_copy(wh.at[:, pl.ds(8192 + i * NC, NC)], DN.at[i, pl.ds(0, D), :], d_sem.at[i])
+
+    def cp_hx(i):
+        if i >= 4:
+            g = i - 4
+            return pltpu.make_async_copy(wh.at[pl.ds(g * 640, 640), pl.ds(10240, D)],
+                                         G.at[g, pl.ds(D, 640), :], x_sem.at[i])
+        return pltpu.make_async_copy(wh.at[pl.ds(1280, 768), pl.ds(10240 + i * NC, NC)],
+                                     DN.at[i, pl.ds(D, 768), :], x_sem.at[i])
 
     ins = [pltpu.make_async_copy(a, b, in_sem.at[i]) for i, (a, b) in enumerate(
         ((hid_h, hid), (lens_h, lens), (ga_h, ga), (gf_h, gf), (gl_h, gl)))]
@@ -146,10 +155,14 @@
         al(j, chip_row).start()
         ad(j, own_n(j)).start()
 
-    def gather_finish():
-        for j in range(2):
+    def gather_finish(*work):
+        for j in range(2):
+            if work:
+                work[j]()
             al(j, oth_row).wait_recv()
             af(j, own_n(j)).start()
+        if work:
+            work[2]()
         for j in range(2):
             ad(j, par_n(j)).wait_recv()
         for j in range(2):
@@ -263,7 +276,26 @@
         if l + 1 == LAYERS:
             for i in range(8):
                 cp_hs(i).start()
-        gather_finish()
+
+        def flip(k):
+            w, j = k % 2, k // 2
+            cp_g(l, k).wait()
+
+            def step(i, carry):
+                row = pl.multiple_of(j * NC + i * 256, 256)
+                for q in range(8):
+                    G[w, pl.ds(row, 256), q * 256:(q + 1) * 256] = G[w, pl.ds(row, 256), q * 256:(q + 1) * 256].T
+                return carry
+
+            lax.fori_loop(0, 2, step, 0)
+
+        def flips(a, b):
+            def work():
+                for k in range(a, b):
+                    flip(k)
+            return work
+
+        gather_finish(flips(0, 7), flips(7, 9), flips(9, 10))
 
         for r in range(4):
             norm_to_h(r * ROWS, ROWS, r * ROWS, gf[l:l + 1, :])
@@ -272,7 +304,7 @@
                 cp_wq(l + 1, i).start()
             for i in range(4):
                 cp_kv(l + 1, i).start()
-        for i in range(12):
+        for i in range(10, 12):
             cp_g(l, i).wait()
 
         def ffn_cols(n0, size):
@@ -283,7 +315,17 @@
             A[:, pl.ds(n0, size)] = (jax.nn.silu(g_) * u_).astype(BF16)
 
         def ffn_step(n, carry):
-            ffn_cols(pl.multiple_of(n * NC, NC), NC)
+            for half in range(2):
+                row = pl.multiple_of(n * NC + half * 256, 256)
+                gu = []
+                for w in range(2):
+                    acc = None
+                    for q in range(8):
+                        t = jnp.dot(H[:, q * 256:(q + 1) * 256], G[w, pl.ds(row, 256), q * 256:(q + 1) * 256],
+                                    preferred_element_type=F32)
+                        acc = t if acc is None else acc + t
+                    gu.append(acc)
+                A[:, pl.ds(row, 256)] = (jax.nn.silu(gu[0]) * gu[1]).astype(BF16)
             return carry
 
         lax.fori_loop(0, 5, ffn_step, 0)
@@ -294,6 +336,8 @@
         else:
             for i in range(8):
                 cp_hg(i).start()
+            for i in range(4, 6):
+                cp_hx(i).start()
 
         def ps(j):
             return rdma(PS.at[j], R1.at[j], p_ss.at[j], p_rs.at[j], partner)
@@ -308,6 +352,7 @@
                 cp_d(l + 1, i).start()
             else:
                 cp_hd(i).start()
+                cp_hx(i).start()
             return y
 
         def chip_sum(j):
@@ -351,11 +396,14 @@
         cp_hg(i).wait()
     for i in range(4):
         cp_hd(i).wait()
+        cp_hx(i).wait()
+    for i in range(4, 6):
+        cp_hx(i).wait()
 
 
 RING = 4
 BLOCKS = VOCAB // NC
-HELD = 20
+HELD = 24
 STREAM = BLOCKS - HELD
 
 
@@ -417,6 +465,14 @@
         stream(t)
         return carry
 
+    def seg_x(t, carry):
+        col = pl.multiple_of((t - 20) * NC, NC)
+        held(t, lambda: dot(H[:, 0:640], G[0, D:D + 640, pl.ds(col, NC)])
+             + dot(H[:, 640:1280], G[1, D:D + 640, pl.ds(col, NC)])
+             + dot(H[:, 1280:2048], DN[t - 20, D:D + 768, :]))
+        stream(t)
+        return carry
+
     def seg_w(t, carry):
         stream(t)
         return carry
@@ -424,7 +480,8 @@
     lax.fori_loop(0, 8, seg_s, 0)
     lax.fori_loop(8, 16, seg_g, 0)
     lax.fori_loop(16, 20, seg_d, 0)
-    lax.fori_loop(20, STREAM, seg_w, 0)
+    lax.fori_loop(20, 24, seg_x, 0)
+    lax.fori_loop(24, STREAM, seg_w, 0)
     for o in range(2):
         cp_out(OH, oh_sem, HELD - 2 + o, o).wait()
         cp_out(OS, os_sem, BLOCKS - 2 + o, o).wait()
@@ -467,7 +524,7 @@
         dma((8,)), dma((12,)), dma((4,)), dma((4,)),
         dma((4,)), dma((4,)), dma((2,)), dma((2,)),
         dma((2,)), dma((2,)), dma((2,)), dma((2,)), dma((2,)), dma((2,)),
-        dma((2,)), dma((2,)), dma((2,)), dma((2,)), dma((1,)), dma((1,)),
+        dma((2,)), dma((2,)), dma((2,)), dma((2,)), dma((1,)), dma((1,)), dma((6,)),
     ]
     return pl.pallas_call(
         body,

time: 111 us -> 107 us (0.964)
  Pallas kernels: 111 us -> 107 us
    pallas_call x1, Pallas kernels: 84.3 us -> 81.9 us  [layers_kernel(): pl.pallas_call(body, out_shape=[pltpu.VMEM((ALL, D), BF16), pltpu.VMEM((8...]
    pallas_call x1, Pallas kernels: 26.8 us -> 25.2 us  [head_kernel(): pl.pallas_call(head_body, out_shape=jax.ShapeDtypeStruct((ALL, VOCAB), F3...]
where the time goes in v1:
time: 107 us
  Pallas kernels  107 us (100%)
    pallas_call x1, Pallas kernels, layers_kernel(): pl.pallas_call(body, out_shape=[pltpu.VMEM((ALL, D), BF16), pltpu.VMEM((8...  81.9 us
    pallas_call x1, Pallas kernels, head_kernel(): pl.pallas_call(head_body, out_shape=jax.ShapeDtypeStruct((ALL, VOCAB), F3...  25.2 us

profile of v1, /device:TPU:0, one launch (start us, length us, event | category | flops | bytes accessed | tf_op | source)
XLA Modules:
  0.0 107.3 jit_solution(16945154758331326498)
XLA Ops:
  0.0 81.9 %layers.1 = (bf16[128,2048]{1,0:T(8,128)(2,1)S(1)}, bf16[8,1024,1152]{2,1,0:T(8,128)(2,1)S(1)}, bf16[2,2736,2048]{2,1,0:T(8,128)(2,1)S(1)}, bf16[4,2816,512]{2,1,0:T(8,128)(2,1)S(1)}) custom-call(bf16[32,2048]{1,0:T(8,128)(2,1)} %hid_h.1, s32[32]{0:T(128)} %lens_h.1, f32[2,2048]{1,0:T(2,128)} %ga_h.1, f32[2,2048]{1,0:T(2,128)} %gf_h.1, f32[1,2048]{1,0:T(1,128)} %bitcast.7, ...), custom_call_target="tpu_custom_call" | custom-call | tf_op jit(solution)/shard_map/layers/pallas_call | solution.py:529
  82.0 25.2 %head.1 = f32[128,25600]{1,0:T(8,128)} custom-call(bf16[128,2048]{1,0:T(8,128)(2,1)S(1)} %get-tuple-element.9.H, bf16[8,1024,1152]{2,1,0:T(8,128)(2,1)S(1)} %get-tuple-element.10.S, bf16[2,2736,2048]{2,1,0:T(8,128)(2,1)S(1)} %get-tuple-element.11.G, bf16[4,2816,512]{2,1,0:T(8,128)(2,1)S(1)} %get-tuple-element.12.DN, bf16[2048,25600]{1,0:T(8,128)(2,1)} %wh.3), custom_call_target="tpu_custom_call" | custom-call | tf_op jit(solution)/shard_map/head/pallas_call | solution.py:495

commit v2 on v1

--- a/solution.py
+++ b/solution.py
@@ -191,17 +191,8 @@
                 if p < 2:
                     cp_wq(0, 2 * p + 4).start()
                     cp_wq(0, 2 * p + 5).start()
-                if p == 1:
-                    for i in range(4):
-                        cp_kv(0, i).start()
-                if p == 2:
-                    for i in range(4):
-                        cp_wo(0, i).start()
             r = jnp.dot(H[0:CHIP, 0:1024], S[2 * p], preferred_element_type=F32)
             r = r + jnp.dot(H[0:CHIP, 1024:2048], S[2 * p + 1], preferred_element_type=F32)
-            if l > 0 or p > 1:
-                cp_wo(l, 2 * p).start()
-                cp_wo(l, 2 * p + 1).start()
             r = r.astype(BF16).astype(F32)
             for j in range(2):
                 rj = r[:, j * KV_W:(j + 1) * KV_W]
@@ -212,6 +203,11 @@
                     Qf[t, pl.ds(row, ROWS), :] = v[0:ROWS]
                     Qs[t, (2 * p + j) * ROWS:(2 * p + j + 1) * ROWS, :] = v[ROWS:CHIP]
             q_send(p).start()
+            if l == 0 and p == 1:
+                for i in range(4):
+                    cp_kv(0, i).start()
+        for i in range(8):
+            cp_wo(l, i).start()
         for p in range(4):
             q_recv(p).wait_recv()
         for p in range(4):
@@ -224,9 +220,6 @@
 
         for g in range(4):
             cp_kv(l, g).wait()
-            if l == 0 and g > 0:
-                for i in range(4):
-                    cp_g(0, 4 * (g - 1) + i).start()
             sc = []
             for i in range(8):
                 b = g * 8 + i
@@ -250,6 +243,12 @@
                         O16[h, r0:r0 + 16, t * 128:(t + 1) * 128] = (
                             Qf[t, h * ROWS + r0:h * ROWS + r0 + 16, :].astype(BF16))
                 o_send(g // 2).start()
+        if l == 0:
+            for i in range(4):
+                cp_g(0, i).start()
+        else:
+            for i in range(4):
+                cp_d(l, i).start()
         for g2 in range(2):
             r0 = g2 * 16
             ref = O16.at[:, pl.ds(ROWS + r0, 16), :]
@@ -259,9 +258,6 @@
 
         for i in range(8):
             cp_wo(l, i).wait()
-        if l == 0:
-            for i in range(4):
-                cp_d(0, i).start()
         for j in range(2):
             acc = None
             for k in range(8):
@@ -273,9 +269,9 @@
             X[n, pl.ds(my_row, ROWS), :] = (X[n, pl.ds(my_row, ROWS), :].astype(F32) + acc[0:ROWS]).astype(BF16)
             X[n, pl.ds(pa_row, ROWS), :] = (X[n, pl.ds(pa_row, ROWS), :].astype(F32) + acc[ROWS:CHIP]).astype(BF16)
             gather_start(j)
-        if l + 1 == LAYERS:
-            for i in range(8):
-                cp_hs(i).start()
+        if l == 0:
+            for i in range(4, 12):
+                cp_g(0, i).start()
 
         def flip(k):
             w, j = k % 2, k // 2
@@ -295,15 +291,22 @@
                     flip(k)
             return work
 
-        gather_finish(flips(0, 7), flips(7, 9), flips(9, 10))
+        def rest():
+            if l == 0:
+                for i in range(4):
+                    cp_d(0, i).start()
+            flip(9)
+
+        gather_finish(flips(0, 7), flips(7, 9), rest)
 
         for r in range(4):
             norm_to_h(r * ROWS, ROWS, r * ROWS, gf[l:l + 1, :])
         if l + 1 < LAYERS:
-            for i in range(8):
+            for i in range(4):
                 cp_wq(l + 1, i).start()
-            for i in range(4):
-                cp_kv(l + 1, i).start()
+        else:
+            for i in range(6):
+                cp_hs(i).start()
         for i in range(10, 12):
             cp_g(l, i).wait()
 
@@ -330,14 +333,6 @@
 
         lax.fori_loop(0, 5, ffn_step, 0)
         ffn_cols(5 * NC, FFN - 5 * NC)
-        if l + 1 < LAYERS:
-            for i in range(12):
-                cp_g(l + 1, i).start()
-        else:
-            for i in range(8):
-                cp_hg(i).start()
-            for i in range(4, 6):
-                cp_hx(i).start()
 
         def ps(j):
             return rdma(PS.at[j], R1.at[j], p_ss.at[j], p_rs.at[j], partner)
@@ -347,13 +342,7 @@
 
         def down(i):
             cp_d(l, i).wait()
-            y = jnp.dot(A[...], DN[i], preferred_element_type=F32)
-            if l + 1 < LAYERS:
-                cp_d(l + 1, i).start()
-            else:
-                cp_hd(i).start()
-                cp_hx(i).start()
-            return y
+            return jnp.dot(A[...], DN[i], preferred_element_type=F32)
 
         def chip_sum(j):
             ps(j).wait_recv()
@@ -369,6 +358,20 @@
         CS[1] = down(3)
         chip_sum(1)
         last = l + 1 == LAYERS
+        if last:
+            for i in range(6, 8):
+                cp_hs(i).start()
+            for i in range(8):
+                cp_hg(i).start()
+            for i in range(4, 6):
+                cp_hx(i).start()
+        else:
+            for i in range(4, 8):
+                cp_wq(l + 1, i).start()
+            for i in range(4):
+                cp_kv(l + 1, i).start()
+            for i in range(8):
+                cp_g(l + 1, i).start()
         for j in range(2):
             cs(j).wait_recv()
             n = own_n(j)
@@ -378,6 +381,13 @@
                 gather_start(j)
             else:
                 ad(j, own_n(j)).start()
+        if last:
+            for i in range(4):
+                cp_hd(i).start()
+                cp_hx(i).start()
+        else:
+            for i in range(8, 12):
+                cp_g(l + 1, i).start()
         for j in range(2):
             ps(j).wait_send()
             cs(j).wait_send()

time: 107 us -> 108 us (level)
  no operation moved by 1% of the time
where the time goes in v2:
time: 108 us
  Pallas kernels  108 us (100%)
    pallas_call x1, Pallas kernels, layers_kernel(): pl.pallas_call(body, out_shape=[pltpu.VMEM((ALL, D), BF16), pltpu.VMEM((8...  82.6 us
    pallas_call x1, Pallas kernels, head_kernel(): pl.pallas_call(head_body, out_shape=jax.ShapeDtypeStruct((ALL, VOCAB), F3...  25.2 us

profile of v2, /device:TPU:0, one launch (start us, length us, event | category | flops | bytes accessed | tf_op | source)
XLA Modules:
  0.0 108.0 jit_solution(1900143430050992833)
XLA Ops:
  0.0 82.6 %layers.1 = (bf16[128,2048]{1,0:T(8,128)(2,1)S(1)}, bf16[8,1024,1152]{2,1,0:T(8,128)(2,1)S(1)}, bf16[2,2736,2048]{2,1,0:T(8,128)(2,1)S(1)}, bf16[4,2816,512]{2,1,0:T(8,128)(2,1)S(1)}) custom-call(bf16[32,2048]{1,0:T(8,128)(2,1)} %hid_h.1, s32[32]{0:T(128)} %lens_h.1, f32[2,2048]{1,0:T(2,128)} %ga_h.1, f32[2,2048]{1,0:T(2,128)} %gf_h.1, f32[1,2048]{1,0:T(1,128)} %bitcast.7, ...), custom_call_target="tpu_custom_call" | custom-call | tf_op jit(solution)/shard_map/layers/pallas_call | solution.py:539
  82.6 25.2 %head.1 = f32[128,25600]{1,0:T(8,128)} custom-call(bf16[128,2048]{1,0:T(8,128)(2,1)S(1)} %get-tuple-element.9.H, bf16[8,1024,1152]{2,1,0:T(8,128)(2,1)S(1)} %get-tuple-element.10.S, bf16[2,2736,2048]{2,1,0:T(8,128)(2,1)S(1)} %get-tuple-element.11.G, bf16[4,2816,512]{2,1,0:T(8,128)(2,1)S(1)} %get-tuple-element.12.DN, bf16[2048,25600]{1,0:T(8,128)(2,1)} %wh.3), custom_call_target="tpu_custom_call" | custom-call | tf_op jit(solution)/shard_map/head/pallas_call | solution.py:505

commit v3 on v1

--- a/solution.py
+++ b/solution.py
@@ -22,6 +22,9 @@
 FFN = 2736
 FFN_PAD = 2816
 NC = 512
+XC = 256
+XN = D // XC
+U = XN // 2
 QH = HEADS * KV_W // 2
 PAIR = 2 * KV_W
 VOCAB = 25600
@@ -33,7 +36,7 @@
 def _rows_norm(chunks, gain, dtype=BF16):
     ss = sum(jnp.sum(v * v, axis=-1, keepdims=True) for v in chunks)
     inv = lax.rsqrt(ss * (1.0 / D) + NORM_EPS)
-    return [(v * inv * gain[:, i * NC:(i + 1) * NC]).astype(dtype) for i, v in enumerate(chunks)]
+    return [(v * inv * gain[:, i * XC:(i + 1) * XC]).astype(dtype) for i, v in enumerate(chunks)]
 
 
 def body(hid_h, lens_h, ga_h, gf_h, gl_h, kv, wq, wo, wg, wu, wd, wh, H, S, G, DN,
@@ -114,8 +117,8 @@
     pl.semaphore_wait(bar, 2)
 
     ins[0].wait()
-    for n in range(4):
-        X[n, pl.ds(my_row, ROWS), :] = hid[:, n * NC:(n + 1) * NC]
+    for n in range(XN):
+        X[n, pl.ds(my_row, ROWS), :] = hid[:, n * XC:(n + 1) * XC]
     hx = rdma(X.at[:, pl.ds(my_row, ROWS), :], X.at[:, pl.ds(my_row, ROWS), :], h_ss.at[0], h_rs.at[0], partner)
     hx.start()
     for i in range(4):
@@ -127,17 +130,17 @@
     rdma(X.at[:, pl.ds(pa_row, ROWS), :], X.at[:, pl.ds(pa_row, ROWS), :], h_ss.at[0], h_rs.at[0], partner).wait_recv()
 
     def x_chunks(row, rows):
-        return [X[n, pl.ds(row, rows), :].astype(F32) for n in range(4)]
+        return [X[n, pl.ds(row, rows), :].astype(F32) for n in range(XN)]
 
     def norm_to_h(row, rows, h_row, gain):
         for n, v in enumerate(_rows_norm(x_chunks(row, rows), gain)):
-            H[pl.ds(h_row, rows), n * NC:(n + 1) * NC] = v
+            H[pl.ds(h_row, rows), n * XC:(n + 1) * XC] = v
 
     def own_n(j):
-        return 2 * c + j
+        return U * c + j
 
     def par_n(j):
-        return 2 * (1 - c) + j
+        return U * (1 - c) + j
 
     def ad(j, n):
         r = X.at[n, pl.ds(chip_row, CHIP), :]
@@ -156,18 +159,18 @@
         ad(j, own_n(j)).start()
 
     def gather_finish(*work):
-        for j in range(2):
+        for j in range(U):
             if work:
                 work[j]()
             al(j, oth_row).wait_recv()
             af(j, own_n(j)).start()
-        if work:
-            work[2]()
-        for j in range(2):
+        for w in work[U:]:
+            w()
+        for j in range(U):
             ad(j, par_n(j)).wait_recv()
-        for j in range(2):
+        for j in range(U):
             af(j, par_n(j)).wait_recv()
-        for j in range(2):
+        for j in range(U):
             al(j, chip_row).wait_send()
             ad(j, own_n(j)).wait_send()
             af(j, own_n(j)).wait_send()
@@ -262,13 +265,16 @@
         if l == 0:
             for i in range(4):
                 cp_d(0, i).start()
-        for j in range(2):
-            acc = None
-            for k in range(8):
-                for hh in range(2):
-                    t = jnp.dot(O16[2 * k + hh], S[k, hh * LATENT:(hh + 1) * LATENT, j * NC:(j + 1) * NC],
+        for j in range(U):
+            acc = []
+            for hh in range(2):
+                a = None
+                for k in range(8):
+                    t = jnp.dot(O16[2 * k + hh], S[k, hh * LATENT:(hh + 1) * LATENT, j * XC:(j + 1) * XC],
                                 preferred_element_type=F32)
-                    acc = t if acc is None else acc + t
+                    a = t if a is None else a + t
+                acc.append(a)
+            acc = acc[0] + acc[1]
             n = own_n(j)
             X[n, pl.ds(my_row, ROWS), :] = (X[n, pl.ds(my_row, ROWS), :].astype(F32) + acc[0:ROWS]).astype(BF16)
             X[n, pl.ds(pa_row, ROWS), :] = (X[n, pl.ds(pa_row, ROWS), :].astype(F32) + acc[ROWS:CHIP]).astype(BF16)
@@ -281,13 +287,9 @@
             w, j = k % 2, k // 2
             cp_g(l, k).wait()
 
-            def step(i, carry):
-                row = pl.multiple_of(j * NC + i * 256, 256)
+            for row in range(j * NC, (j + 1) * NC, 256):
                 for q in range(8):
-                    G[w, pl.ds(row, 256), q * 256:(q + 1) * 256] = G[w, pl.ds(row, 256), q * 256:(q + 1) * 256].T
-                return carry
-
-            lax.fori_loop(0, 2, step, 0)
+                    G[w, row:row + 256, q * 256:(q + 1) * 256] = G[w, row:row + 256, q * 256:(q + 1) * 256].T
 
         def flips(a, b):
             def work():
@@ -295,7 +297,7 @@
                     flip(k)
             return work
 
-        gather_finish(flips(0, 7), flips(7, 9), flips(9, 10))
+        gather_finish(flips(0, 4), flips(4, 6), flips(6, 8), flips(8, 9), flips(9, 10))
 
         for r in range(4):
             norm_to_h(r * ROWS, ROWS, r * ROWS, gf[l:l + 1, :])
@@ -345,31 +347,39 @@
         def cs(j):
             return rdma(CS.at[j, pl.ds(oth_row, CHIP), :], R2.at[j], c_ss.at[j], c_rs.at[j], other)
 
-        def down(i):
-            cp_d(l, i).wait()
-            y = jnp.dot(A[...], DN[i], preferred_element_type=F32)
+        def down(i, half, buf):
+            k = 6 * 256
+            col = half * XC
+            buf[i // 2 * 2 + half] = (
+                jnp.dot(A[:, 0:k], DN[i, 0:k, col:col + XC], preferred_element_type=F32)
+                + jnp.dot(A[:, k:FFN_PAD], DN[i, k:FFN_PAD, col:col + XC], preferred_element_type=F32))
+
+        def next_d(i):
             if l + 1 < LAYERS:
                 cp_d(l + 1, i).start()
             else:
                 cp_hd(i).start()
                 cp_hx(i).start()
-            return y
 
         def chip_sum(j):
             ps(j).wait_recv()
             CS[j] = CS[j] + R1[j]
             cs(j).start()
 
-        PS[0] = down(0)
-        ps(0).start()
-        CS[0] = down(1)
-        PS[1] = down(2)
-        ps(1).start()
-        chip_sum(0)
-        CS[1] = down(3)
-        chip_sum(1)
+        for i in range(4):
+            cp_d(l, i).wait()
+            for half in range(2):
+                if i % 2 == 0:
+                    down(i, half, PS)
+                    ps(i + half).start()
+                else:
+                    down(i, half, CS)
+            next_d(i)
+            if i >= 2:
+                for j in (2 * i - 4, 2 * i - 3):
+                    chip_sum(j)
         last = l + 1 == LAYERS
-        for j in range(2):
+        for j in range(U):
             cs(j).wait_recv()
             n = own_n(j)
             xr = X[n, pl.ds(chip_row, CHIP), :].astype(F32)
@@ -378,15 +388,15 @@
                 gather_start(j)
             else:
                 ad(j, own_n(j)).start()
-        for j in range(2):
+        for j in range(U):
             ps(j).wait_send()
             cs(j).wait_send()
         if last:
             gather_finish()
         else:
-            for j in range(2):
+            for j in range(U):
                 ad(j, par_n(j)).wait_recv()
-            for j in range(2):
+            for j in range(U):
                 ad(j, own_n(j)).wait_send()
 
     for r in range(4):
@@ -512,19 +522,19 @@
         pltpu.VMEM((ROWS, D), BF16), pltpu.SMEM((ROWS,), jnp.int32), pltpu.VMEM((2, D), F32), pltpu.VMEM((2, D), F32),
         pltpu.VMEM((1, D), F32), dma((5,)),
         pltpu.VMEM((ROWS, KV_W, SEQ), BF16),
-        pltpu.VMEM((4, ALL, NC), BF16),
+        pltpu.VMEM((XN, ALL, XC), BF16),
         pltpu.VMEM((5, HEADS * ROWS, 128), F32),
         pltpu.VMEM((5, 8 * ROWS, 128), F32),
         pltpu.VMEM((HEADS, CHIP, LATENT), BF16),
         pltpu.VMEM((ALL, FFN_PAD), BF16),
-        pltpu.VMEM((2, ALL, NC), F32),
-        pltpu.VMEM((2, ALL, NC), F32),
-        pltpu.VMEM((2, ALL, NC), F32),
-        pltpu.VMEM((2, CHIP, NC), F32),
+        pltpu.VMEM((U, ALL, XC), F32),
+        pltpu.VMEM((U, ALL, XC), F32),
+        pltpu.VMEM((U, ALL, XC), F32),
+        pltpu.VMEM((U, CHIP, XC), F32),
         dma((8,)), dma((12,)), dma((4,)), dma((4,)),
         dma((4,)), dma((4,)), dma((2,)), dma((2,)),
-        dma((2,)), dma((2,)), dma((2,)), dma((2,)), dma((2,)), dma((2,)),
-        dma((2,)), dma((2,)), dma((2,)), dma((2,)), dma((1,)), dma((1,)), dma((6,)),
+        dma((U,)), dma((U,)), dma((U,)), dma((U,)), dma((U,)), dma((U,)),
+        dma((U,)), dma((U,)), dma((U,)), dma((U,)), dma((1,)), dma((1,)), dma((6,)),
     ]
     return pl.pallas_call(
         body,

time: 107 us -> 112 us (1.047)
  Pallas kernels: 107 us -> 112 us
    pallas_call x1, Pallas kernels: 81.9 us -> 86.8 us  [layers_kernel(): pl.pallas_call(body, out_shape=[pltpu.VMEM((ALL, D), BF16), pltpu.VMEM((8...]
where the time goes in v3:
time: 112 us
  Pallas kernels  112 us (100%)
    pallas_call x1, Pallas kernels, layers_kernel(): pl.pallas_call(body, out_shape=[pltpu.VMEM((ALL, D), BF16), pltpu.VMEM((8...  86.8 us
    pallas_call x1, Pallas kernels, head_kernel(): pl.pallas_call(head_body, out_shape=jax.ShapeDtypeStruct((ALL, VOCAB), F3...  25.2 us

profile of v3, /device:TPU:0, one launch (start us, length us, event | category | flops | bytes accessed | tf_op | source)
XLA Modules:
  0.0 112.1 jit_solution(13512382684648776905)
XLA Ops:
  0.0 86.8 %layers.1 = (bf16[128,2048]{1,0:T(8,128)(2,1)S(1)}, bf16[8,1024,1152]{2,1,0:T(8,128)(2,1)S(1)}, bf16[2,2736,2048]{2,1,0:T(8,128)(2,1)S(1)}, bf16[4,2816,512]{2,1,0:T(8,128)(2,1)S(1)}) custom-call(bf16[32,2048]{1,0:T(8,128)(2,1)} %hid_h.1, s32[32]{0:T(128)} %lens_h.1, f32[2,2048]{1,0:T(2,128)} %ga_h.1, f32[2,2048]{1,0:T(2,128)} %gf_h.1, f32[1,2048]{1,0:T(1,128)} %bitcast.7, ...), custom_call_target="tpu_custom_call" | custom-call | tf_op jit(solution)/shard_map/layers/pallas_call | solution.py:539
  86.8 25.2 %head.1 = f32[128,25600]{1,0:T(8,128)} custom-call(bf16[128,2048]{1,0:T(8,128)(2,1)S(1)} %get-tuple-element.9.H, bf16[8,1024,1152]{2,1,0:T(8,128)(2,1)S(1)} %get-tuple-element.10.S, bf16[2,2736,2048]{2,1,0:T(8,128)(2,1)S(1)} %get-tuple-element.11.G, bf16[4,2816,512]{2,1,0:T(8,128)(2,1)S(1)} %get-tuple-element.12.DN, bf16[2048,25600]{1,0:T(8,128)(2,1)} %wh.3), custom_call_target="tpu_custom_call" | custom-call | tf_op jit(solution)/shard_map/head/pallas_call | solution.py:505

commit v4 on v1

--- a/solution.py
+++ b/solution.py
@@ -281,13 +281,9 @@
             w, j = k % 2, k // 2
             cp_g(l, k).wait()
 
-            def step(i, carry):
-                row = pl.multiple_of(j * NC + i * 256, 256)
+            for row in range(j * NC, (j + 1) * NC, 256):
                 for q in range(8):
-                    G[w, pl.ds(row, 256), q * 256:(q + 1) * 256] = G[w, pl.ds(row, 256), q * 256:(q + 1) * 256].T
-                return carry
-
-            lax.fori_loop(0, 2, step, 0)
+                    G[w, row:row + 256, q * 256:(q + 1) * 256] = G[w, row:row + 256, q * 256:(q + 1) * 256].T
 
         def flips(a, b):
             def work():
@@ -295,7 +291,7 @@
                     flip(k)
             return work
 
-        gather_finish(flips(0, 7), flips(7, 9), flips(9, 10))
+        gather_finish(flips(0, 5), flips(5, 8), flips(8, 10))
 
         for r in range(4):
             norm_to_h(r * ROWS, ROWS, r * ROWS, gf[l:l + 1, :])
@@ -401,75 +397,84 @@
         cp_hx(i).wait()
 
 
-RING = 4
-BLOCKS = VOCAB // NC
-HELD = 24
+HB = 1024
+RING = 2
+BLOCKS = VOCAB // HB
+HELD = 12
 STREAM = BLOCKS - HELD
 
 
 def head_body(H, S, G, DN, wh, out, W, OH, OS, w_sem, oh_sem, os_sem):
-    def cp_w(t, slot):
-        col = pl.multiple_of((HELD + t) * NC, NC)
-        return pltpu.make_async_copy(wh.at[:, pl.ds(col, NC)], W.at[slot], w_sem.at[slot])
-
-    def cp_out(buf, sems, block, slot):
-        col = pl.multiple_of(block * NC, NC)
-        return pltpu.make_async_copy(buf.at[slot], out.at[:, pl.ds(col, NC)], sems.at[slot])
+    def cp_w(t, slot, k):
+        col = pl.multiple_of((HELD + t) * HB, HB)
+        return pltpu.make_async_copy(wh.at[pl.ds(k * 1024, 1024), pl.ds(col, HB)], W.at[slot, k], w_sem.at[slot, k])
+
+    def cp_out(buf, sem, block):
+        col = pl.multiple_of(block * HB, HB)
+        return pltpu.make_async_copy(buf, out.at[:, pl.ds(col, HB)], sem)
 
     for t in range(RING):
-        cp_w(t, t).start()
+        for k in range(2):
+            cp_w(t, t, k).start()
+
+    def dot(a, b):
+        return jnp.dot(a, b, preferred_element_type=F32)
 
     def stream(t):
-        slot, o = lax.rem(t, RING), lax.rem(t, 2)
-        cp_w(t, slot).wait()
+        slot = lax.rem(t, RING)
+        cp_w(t, slot, 0).wait()
+        cp_w(t, slot, 1).wait()
 
         @pl.when(t >= 2)
         def _():
-            cp_out(OS, os_sem, HELD + t, o).wait()
-
-        OS[o] = jnp.dot(H[...], W[slot], preferred_element_type=F32)
-        cp_out(OS, os_sem, HELD + t, o).start()
+            cp_out(OS.at[slot], os_sem.at[slot], HELD + t).wait()
+
+        for i in range(2):
+            cols = slice(i * NC, (i + 1) * NC)
+            OS[slot, :, cols] = dot(H[:, 0:1024], W[slot, 0, :, cols]) + dot(H[:, 1024:2048], W[slot, 1, :, cols])
 
         @pl.when(t + RING < STREAM)
         def _():
-            cp_w(t + RING, slot).start()
-
-    def held(t, value):
-        o = lax.rem(t, 2)
-
-        @pl.when(t >= 2)
+            cp_w(t + RING, slot, 0).start()
+            cp_w(t + RING, slot, 1).start()
+
+        cp_out(OS.at[slot], os_sem.at[slot], HELD + t).start()
+
+    def held(t, *values):
+        @pl.when(t >= 1)
         def _():
-            cp_out(OH, oh_sem, t, o).wait()
-
-        OH[o] = value()
-        cp_out(OH, oh_sem, t, o).start()
-
-    def dot(a, b):
-        return jnp.dot(a, b, preferred_element_type=F32)
+            cp_out(OH, oh_sem.at[0], t).wait()
+
+        width = HB // len(values)
+        for i, value in enumerate(values):
+            OH[:, i * width:(i + 1) * width] = value()
+        cp_out(OH, oh_sem.at[0], t).start()
 
     def seg_s(t, carry):
-        p, col = t // 2, pl.multiple_of(lax.rem(t, 2) * NC, NC)
-        held(t, lambda: dot(H[:, 0:1024], S[2 * p, :, pl.ds(col, NC)])
-             + dot(H[:, 1024:2048], S[2 * p + 1, :, pl.ds(col, NC)]))
+        held(t, *[lambda i=i: dot(H[:, 0:1024], S[2 * t, :, i * NC:(i + 1) * NC])
+                  + dot(H[:, 1024:2048], S[2 * t + 1, :, i * NC:(i + 1) * NC]) for i in range(2)])
         stream(t)
         return carry
 
     def seg_g(t, carry):
-        g, col = t // 4 - 2, pl.multiple_of(lax.rem(t, 4) * NC, NC)
-        held(t, lambda: dot(H[...], G[g, 0:D, pl.ds(col, NC)]))
+        g, col = t // 2 - 2, lax.rem(t, 2) * HB
+        held(t, *[lambda i=i: dot(H[...], G[g, 0:D, pl.ds(pl.multiple_of(col + i * NC, NC), NC)]) for i in range(2)])
         stream(t)
         return carry
 
     def seg_d(t, carry):
-        held(t, lambda: dot(H[...], DN[t - 16, 0:D, :]))
+        held(t, *[lambda i=i: dot(H[...], DN[2 * (t - 8) + i, 0:D, :]) for i in range(2)])
         stream(t)
         return carry
 
     def seg_x(t, carry):
-        col = pl.multiple_of((t - 20) * NC, NC)
-        held(t, lambda: dot(H[:, 0:640], G[0, D:D + 640, pl.ds(col, NC)])
-             + dot(H[:, 640:1280], G[1, D:D + 640, pl.ds(col, NC)])
-             + dot(H[:, 1280:2048], DN[t - 20, D:D + 768, :]))
+        def part(i):
+            col = pl.multiple_of((t - 10) * HB + i * NC, NC)
+            return (dot(H[:, 0:640], G[0, D:D + 640, pl.ds(col, NC)])
+                    + dot(H[:, 640:1280], G[1, D:D + 640, pl.ds(col, NC)])
+                    + dot(H[:, 1280:2048], DN[2 * (t - 10) + i, D:D + 768, :]))
+
+        held(t, lambda: part(0), lambda: part(1))
         stream(t)
         return carry
 
@@ -477,14 +482,15 @@
         stream(t)
         return carry
 
-    lax.fori_loop(0, 8, seg_s, 0)
-    lax.fori_loop(8, 16, seg_g, 0)
-    lax.fori_loop(16, 20, seg_d, 0)
-    lax.fori_loop(20, 24, seg_x, 0)
-    lax.fori_loop(24, STREAM, seg_w, 0)
+    lax.fori_loop(0, 4, seg_s, 0)
+    lax.fori_loop(4, 8, seg_g, 0)
+    lax.fori_loop(8, 10, seg_d, 0)
+    lax.fori_loop(10, 12, seg_x, 0)
+    lax.fori_loop(12, STREAM, seg_w, 0)
+    cp_out(OH, oh_sem.at[0], HELD - 1).wait()
     for o in range(2):
-        cp_out(OH, oh_sem, HELD - 2 + o, o).wait()
-        cp_out(OS, os_sem, BLOCKS - 2 + o, o).wait()
+        t = STREAM - 2 + o
+        cp_out(OS.at[t % 2], os_sem.at[t % 2], HELD + t).wait()
 
 
 def head_kernel(normed, s_buf, g_buf, d_buf, w_head):
@@ -497,8 +503,8 @@
         out_shape=jax.ShapeDtypeStruct((ALL, VOCAB), F32),
         in_specs=[vm] * 4 + [hb],
         out_specs=hb,
-        scratch_shapes=[pltpu.VMEM((RING, D, NC), BF16), pltpu.VMEM((2, ALL, NC), F32), pltpu.VMEM((2, ALL, NC), F32),
-                        dma((RING,)), dma((2,)), dma((2,))],
+        scratch_shapes=[pltpu.VMEM((RING, 2, 1024, HB), BF16), pltpu.VMEM((ALL, HB), F32), pltpu.VMEM((2, ALL, HB), F32),
+                        dma((RING, 2)), dma((1,)), dma((2,))],
         compiler_params=pltpu.CompilerParams(vmem_limit_bytes=13500000),
         name='head',
     )(*held, w_head)

time: 107 us -> 105 us (0.981)
  Pallas kernels: 107 us -> 104 us
    pallas_call x1, Pallas kernels: 81.9 us -> 80.4 us  [layers_kernel(): pl.pallas_call(body, out_shape=[pltpu.VMEM((ALL, D), BF16), pltpu.VMEM((8...]
    pallas_call x1, Pallas kernels: 25.2 us -> 24.1 us  [head_kernel(): pl.pallas_call(head_body, out_shape=jax.ShapeDtypeStruct((ALL, VOCAB), F3...]
where the time goes in v4:
time: 105 us
  Pallas kernels  104 us (99%)
    pallas_call x1, Pallas kernels, layers_kernel(): pl.pallas_call(body, out_shape=[pltpu.VMEM((ALL, D), BF16), pltpu.VMEM((8...  80.4 us
    pallas_call x1, Pallas kernels, head_kernel(): pl.pallas_call(head_body, out_shape=jax.ShapeDtypeStruct((ALL, VOCAB), F3...  24.1 us

profile of v4, /device:TPU:0, one launch (start us, length us, event | category | flops | bytes accessed | tf_op | source)
XLA Modules:
  0.0 104.6 jit_solution(4673063064235508376)
XLA Ops:
  0.0 80.4 %layers.1 = (bf16[128,2048]{1,0:T(8,128)(2,1)S(1)}, bf16[8,1024,1152]{2,1,0:T(8,128)(2,1)S(1)}, bf16[2,2736,2048]{2,1,0:T(8,128)(2,1)S(1)}, bf16[4,2816,512]{2,1,0:T(8,128)(2,1)S(1)}) custom-call(bf16[32,2048]{1,0:T(8,128)(2,1)} %hid_h.1, s32[32]{0:T(128)} %lens_h.1, f32[2,2048]{1,0:T(2,128)} %ga_h.1, f32[2,2048]{1,0:T(2,128)} %gf_h.1, f32[1,2048]{1,0:T(1,128)} %bitcast.7, ...), custom_call_target="tpu_custom_call" | custom-call | tf_op jit(solution)/shard_map/layers/pallas_call | solution.py:535
  80.4 24.1 %head.1 = f32[128,25600]{1,0:T(8,128)} custom-call(bf16[128,2048]{1,0:T(8,128)(2,1)S(1)} %get-tuple-element.9.H, bf16[8,1024,1152]{2,1,0:T(8,128)(2,1)S(1)} %get-tuple-element.10.S, bf16[2,2736,2048]{2,1,0:T(8,128)(2,1)S(1)} %get-tuple-element.11.G, bf16[4,2816,512]{2,1,0:T(8,128)(2,1)S(1)} %get-tuple-element.12.DN, bf16[2048,25600]{1,0:T(8,128)(2,1)} %wh.3), custom_call_target="tpu_custom_call" | custom-call | tf_op jit(solution)/shard_map/head/pallas_call | solution.py:501

commit v5 on v4

--- a/solution.py
+++ b/solution.py
@@ -155,7 +155,7 @@
         al(j, chip_row).start()
         ad(j, own_n(j)).start()
 
-    def gather_finish(*work):
+    def gather_finish(gain, *work):
         for j in range(2):
             if work:
                 work[j]()
@@ -165,8 +165,14 @@
             work[2]()
         for j in range(2):
             ad(j, par_n(j)).wait_recv()
+        for r in range(2):
+            row = pl.multiple_of(chip_row + r * ROWS, ROWS)
+            norm_to_h(row, ROWS, row, gain)
         for j in range(2):
             af(j, par_n(j)).wait_recv()
+        for r in range(2):
+            row = pl.multiple_of(oth_row + r * ROWS, ROWS)
+            norm_to_h(row, ROWS, row, gain)
         for j in range(2):
             al(j, chip_row).wait_send()
             ad(j, own_n(j)).wait_send()
@@ -222,34 +228,38 @@
             return rdma(O16.at[:, pl.ds(r0, 16), :], O16.at[:, pl.ds(ROWS + r0, 16), :],
                         o_ss.at[g2], o_rs.at[g2], partner)
 
-        for g in range(4):
-            cp_kv(l, g).wait()
-            if l == 0 and g > 0:
-                for i in range(4):
-                    cp_g(0, 4 * (g - 1) + i).start()
-            sc = []
-            for i in range(8):
-                b = g * 8 + i
-                qb = jnp.concatenate([Qf[t, pl.ds(b, HEADS, stride=ROWS), :] for t in range(5)], axis=1)
-                s = jnp.dot(qb[:, 0:KV_W].astype(BF16), KV[b], preferred_element_type=F32) * QK_SCALE
-                pos = lax.broadcasted_iota(jnp.int32, (HEADS, SEQ), 1)
-                sc.append(jnp.where(pos < lens[b], s, -1e30))
-            s = jnp.concatenate(sc, axis=0)
-            e = jnp.exp(s - jnp.max(s, axis=-1, keepdims=True))
-            pr = (e / jnp.sum(e, axis=-1, keepdims=True)).astype(BF16)
-            for i in range(8):
-                b = g * 8 + i
-                o = lax.dot_general(pr[i * HEADS:(i + 1) * HEADS], KV[b, 0:LATENT, :], (((1,), (1,)), ((), ())),
-                                    preferred_element_type=F32)
+        for g2 in range(2):
+            prs = []
+            for g in (2 * g2, 2 * g2 + 1):
+                cp_kv(l, g).wait()
+                if l == 0 and g > 0:
+                    for i in range(4):
+                        cp_g(0, 4 * (g - 1) + i).start()
+            for g in (2 * g2, 2 * g2 + 1):
+                sc = []
+                for i in range(8):
+                    b = g * 8 + i
+                    qb = jnp.concatenate([Qf[t, pl.ds(b, HEADS, stride=ROWS), :] for t in range(5)], axis=1)
+                    s = jnp.dot(qb[:, 0:KV_W].astype(BF16), KV[b], preferred_element_type=F32) * QK_SCALE
+                    pos = lax.broadcasted_iota(jnp.int32, (HEADS, SEQ), 1)
+                    sc.append(jnp.where(pos < lens[b], s, -1e30))
+                s = jnp.concatenate(sc, axis=0)
+                e = jnp.exp(s - jnp.max(s, axis=-1, keepdims=True))
+                prs.append((e / jnp.sum(e, axis=-1, keepdims=True)).astype(BF16))
+            for g in (2 * g2, 2 * g2 + 1):
+                pr = prs[g % 2]
+                for i in range(8):
+                    b = g * 8 + i
+                    o = lax.dot_general(pr[i * HEADS:(i + 1) * HEADS], KV[b, 0:LATENT, :], (((1,), (1,)), ((), ())),
+                                        preferred_element_type=F32)
+                    for t in range(4):
+                        Qf[t, pl.ds(b, HEADS, stride=ROWS), :] = o[:, t * 128:(t + 1) * 128]
+            r0 = g2 * 16
+            for h in range(HEADS):
                 for t in range(4):
-                    Qf[t, pl.ds(b, HEADS, stride=ROWS), :] = o[:, t * 128:(t + 1) * 128]
-            if g % 2 == 1:
-                r0 = (g // 2) * 16
-                for h in range(HEADS):
-                    for t in range(4):
-                        O16[h, r0:r0 + 16, t * 128:(t + 1) * 128] = (
-                            Qf[t, h * ROWS + r0:h * ROWS + r0 + 16, :].astype(BF16))
-                o_send(g // 2).start()
+                    O16[h, r0:r0 + 16, t * 128:(t + 1) * 128] = (
+                        Qf[t, h * ROWS + r0:h * ROWS + r0 + 16, :].astype(BF16))
+            o_send(g2).start()
         for g2 in range(2):
             r0 = g2 * 16
             ref = O16.at[:, pl.ds(ROWS + r0, 16), :]
@@ -291,10 +301,8 @@
                     flip(k)
             return work
 
-        gather_finish(flips(0, 5), flips(5, 8), flips(8, 10))
-
-        for r in range(4):
-            norm_to_h(r * ROWS, ROWS, r * ROWS, gf[l:l + 1, :])
+        gather_finish(gf[l:l + 1, :], flips(0, 5), flips(5, 8), flips(8, 10))
+
         if l + 1 < LAYERS:
             for i in range(8):
                 cp_wq(l + 1, i).start()
@@ -378,15 +386,13 @@
             ps(j).wait_send()
             cs(j).wait_send()
         if last:
-            gather_finish()
+            gather_finish(gl[...])
         else:
             for j in range(2):
                 ad(j, par_n(j)).wait_recv()
             for j in range(2):
                 ad(j, own_n(j)).wait_send()
 
-    for r in range(4):
-        norm_to_h(r * ROWS, ROWS, r * ROWS, gl[...])
     for i in range(8):
         cp_hs(i).wait()
         cp_hg(i).wait()

time: 105 us -> 104 us (level)
  no operation moved by 1% of the time
where the time goes in v5:
time: 104 us
  Pallas kernels  104 us (100%)
    pallas_call x1, Pallas kernels, layers_kernel(): pl.pallas_call(body, out_shape=[pltpu.VMEM((ALL, D), BF16), pltpu.VMEM((8...  79.9 us
    pallas_call x1, Pallas kernels, head_kernel(): pl.pallas_call(head_body, out_shape=jax.ShapeDtypeStruct((ALL, VOCAB), F3...  24.1 us

profile of v5, /device:TPU:0, one launch (start us, length us, event | category | flops | bytes accessed | tf_op | source)
XLA Modules:
  0.0 104.2 jit_solution(1003660313714458664)
XLA Ops:
  0.0 79.9 %layers.1 = (bf16[128,2048]{1,0:T(8,128)(2,1)S(1)}, bf16[8,1024,1152]{2,1,0:T(8,128)(2,1)S(1)}, bf16[2,2736,2048]{2,1,0:T(8,128)(2,1)S(1)}, bf16[4,2816,512]{2,1,0:T(8,128)(2,1)S(1)}) custom-call(bf16[32,2048]{1,0:T(8,128)(2,1)} %hid_h.1, s32[32]{0:T(128)} %lens_h.1, f32[2,2048]{1,0:T(2,128)} %ga_h.1, f32[2,2048]{1,0:T(2,128)} %gf_h.1, f32[1,2048]{1,0:T(1,128)} %bitcast.7, ...), custom_call_target="tpu_custom_call" | custom-call | tf_op jit(solution)/shard_map/layers/pallas_call | solution.py:541
  79.9 24.1 %head.1 = f32[128,25600]{1,0:T(8,128)} custom-call(bf16[128,2048]{1,0:T(8,128)(2,1)S(1)} %get-tuple-element.9.H, bf16[8,1024,1152]{2,1,0:T(8,128)(2,1)S(1)} %get-tuple-element.10.S, bf16[2,2736,2048]{2,1,0:T(8,128)(2,1)S(1)} %get-tuple-element.11.G, bf16[4,2816,512]{2,1,0:T(8,128)(2,1)S(1)} %get-tuple-element.12.DN, bf16[2048,25600]{1,0:T(8,128)(2,1)} %wh.3), custom_call_target="tpu_custom_call" | custom-call | tf_op jit(solution)/shard_map/head/pallas_call | solution.py:507
